TPU v7x, 32 devices: a whole 2x2x4 slice. The times are simulated.
32 devices in a mesh: grp: 1, exp: 32 (over z, y, x, core).
Axes of the slice: x: 2, y: 2, z: 4, core: 2. Of those that a mesh axis runs over, the one named last changes fastest.
Arguments:
- tokens: bfloat16 [512, 2048], P(('grp', 'exp')), may hold values from -6 to 6
- routed_expert_index: int32 [512, 6], P(('grp', 'exp')), may hold values from 0 to 15, all different within a row; in each aligned block of 16 rows (0 to 15, 16 to 31, ...) at most 8 rows name the same one
- routing_gate_weight: float32 [512, 6], P(('grp', 'exp')), may hold values from 0.05 to 0.5
- token_adapter_index: int32 [512], P('grp'), may hold values from 0 to 511
- gate_weight_pieces: bfloat16 [32, 2048, 704], P('exp'), may hold values from -0.125 to 0.125
- up_weight: bfloat16 [32, 2048, 704], P('exp'), may hold values from -0.125 to 0.125
- down_weight: bfloat16 [32, 704, 2048], P('exp'), may hold values from -0.15625 to 0.15625
- adapter_down_matrix: bfloat16 [2048, 8192], P('exp'), may hold values from -0.125 to 0.125
- adapter_up_matrix: bfloat16 [2048, 8192], P('exp'), may hold values from -1.5 to 1.5
Outputs:
- mixed: bfloat16 [512, 2048], P(('grp', 'exp'))
Inputs may be any that keep to these rules, and one draw needn't show every extreme that they name: `routed_expert_index`: each token names 6 different experts; among the 16 tokens of one index of exp (aligned blocks of rows) no expert is named more than 8 times.
All inputs are finite; a program needn't handle non-finite values.
Results may differ from a plain program's by a relative error of at most 0.009.
Values may be sent and summed in bfloat16 or wider, within the bound.
A program may use at most 128 MiB of HBM per device.

v0:
```python
import jax
import jax.numpy as jnp
from jax import lax
from jax.sharding import PartitionSpec as P

TOP = 6
ADAPTER_RANK = 16


def expert_half(row_block, gate_weight_pieces, up_weight, down_weight):
    gate_act = jnp.dot(row_block, gate_weight_pieces[0], preferred_element_type=jnp.float32)
    up_act = jnp.dot(row_block, up_weight[0], preferred_element_type=jnp.float32)
    hidden = (jax.nn.silu(gate_act) * up_act).astype(jnp.bfloat16)
    return jnp.dot(hidden, down_weight[0], preferred_element_type=jnp.float32)


def per_device(
    tokens,
    routed_expert_index,
    routing_gate_weight,
    token_adapter_index,
    gate_weight_pieces,
    up_weight,
    down_weight,
    adapter_down_matrix,
    adapter_up_matrix,
):
    devices = lax.axis_size("exp")
    experts = devices // 2
    tok_dev = tokens.shape[0]
    model_width = tokens.shape[1]
    capacity = 2 * (tok_dev * TOP // devices + 1)
    flat_ids = routed_expert_index.reshape(-1)
    gate_col = routing_gate_weight.reshape(-1, 1)
    one_hot = (flat_ids[:, None] == jnp.arange(experts, dtype=jnp.int32)[None, :]).astype(jnp.int32)
    counted = jnp.cumsum(one_hot, axis=0)
    position = jnp.sum(one_hot * counted, axis=1) - 1
    slots = flat_ids * capacity + position
    token_rows = jnp.repeat(tokens, TOP, axis=0)
    buffer = jnp.zeros((experts * capacity, model_width), tokens.dtype).at[slots].set(token_rows)
    buffer, slots = (buffer, slots)
    doubled = jnp.broadcast_to(
        buffer.reshape(experts, 1, capacity, model_width), (experts, 2, capacity, model_width)
    )
    doubled = doubled.reshape(devices, capacity, model_width)
    received = lax.all_to_all(doubled, "exp", split_axis=0, concat_axis=0, tiled=True)
    sources = received.shape[0]
    items = received.shape[1]
    output = expert_half(
        received.reshape(sources * items, model_width), gate_weight_pieces, up_weight, down_weight
    )
    partial_value = output.reshape(sources, items, model_width)
    returned = lax.all_to_all(
        partial_value.astype(jnp.bfloat16), "exp", split_axis=0, concat_axis=0, tiled=True
    ).astype(partial_value.dtype)
    results = jnp.sum(returned.reshape(experts, 2, capacity, model_width), axis=1)
    gather_results = results.reshape(experts * capacity, model_width)
    picked = gather_results[slots] * gate_col
    routed = jnp.sum(picked.reshape(tok_dev, TOP, model_width), axis=1)
    columns = lax.all_to_all(tokens, "exp", split_axis=1, concat_axis=0, tiled=True)
    feature_rows = adapter_down_matrix.shape[0]
    adapter_table = adapter_down_matrix.shape[1] // ADAPTER_RANK
    down_selected = adapter_down_matrix.reshape(feature_rows, adapter_table, ADAPTER_RANK)[
        :, token_adapter_index, :
    ]
    rank_terms = jnp.einsum(
        "tf,ftr->tr", columns, down_selected, preferred_element_type=jnp.float32
    )
    gathered_ranks = lax.psum(rank_terms, "exp").astype(jnp.bfloat16)
    up_selected = adapter_up_matrix.reshape(feature_rows, adapter_table, ADAPTER_RANK)[
        :, token_adapter_index, :
    ]
    correction_cols = jnp.einsum(
        "tr,ftr->tf", gathered_ranks, up_selected, preferred_element_type=jnp.float32
    )
    lowrank_delta = lax.all_to_all(
        correction_cols.astype(jnp.bfloat16), "exp", split_axis=0, concat_axis=1, tiled=True
    )
    return (routed + lowrank_delta.astype(jnp.float32)).astype(jnp.bfloat16)


def solution(mesh):
    placed = (
        P(("grp", "exp"), None),
        P(("grp", "exp"), None),
        P(("grp", "exp"), None),
        P("grp"),
        P("exp", None, None),
        P("exp", None, None),
        P("exp", None, None),
        P("exp", None),
        P("exp", None),
    )
    return jax.shard_map(
        per_device, mesh=mesh, in_specs=placed, out_specs=P(("grp", "exp"), None), check_vma=False
    )
```

profile of v0, /device:TPU:0, one launch (start us, length us, event | category | flops | bytes accessed | tf_op | source)
XLA Modules:
  0.0 140.4 jit_solution(14712672242584712208)
XLA Ops:
  0.0 0.0 copy-start
  0.0 1.2 all_to_all.32
  1.2 0.1 copy.38
  1.2 0.8 reshape.132
  2.0 7.3 %all-to-all-start.2 = ((bf16[32,2,512]{2,1,0:T(2,128)(2,1)}), bf16[32,2,512]{2,1,0:T(2,128)(2,1)S(1)}, u32[]{:S(2)}, u32[]{:S(2)}) async-start(bf16[32,2,512]{2,1,0:T(2,128)(2,1)} %reshape.132), calls=%async_computation.2 | async-start | bytes 131072 | tf_op jit(solution)/shard_map/all_to_all | solution.py:60
  9.3 0.7 broadcast_multiply_fusion
  10.0 0.8 copy.22
  10.8 0.1 copy.21
  10.9 0.1 mul.37
  11.0 0.1 eq.15
  11.1 0.1 fusion.26
  11.2 0.1 reduce_window_sum.11
  11.3 0.2 select_reduce_fusion
  11.5 0.9 broadcast_in_dim.21
  12.4 0.9 reshape.119
  13.3 1.8 %scatter_custom_fusion = bf16[128,2048]{1,0:T(8,128)(2,1)S(1)} fusion(s32[96]{0:T(128)S(1)} %fusion.27, bf16[96,2048]{1,0:T(8,128)(2,1)} %reshape.119, bf16[]{:T(256)} %constant.8.clone.1), kind=kCustom, calls=%fused_computation.25 | custom fusion | bytes 524800 | tf_op jit(solution)/shard_map/scatter | solution.py:40
  15.1 1.7 %all-to-all-done.2 = bf16[32,2,512]{2,1,0:T(2,128)(2,1)S(1)} async-done(((bf16[32,2,512]{2,1,0:T(2,128)(2,1)}), bf16[32,2,512]{2,1,0:T(2,128)(2,1)S(1)}, u32[]{:S(2)}, u32[]{:S(2)}) %all-to-all-start.2) | async-done | bytes 65568 | tf_op jit(solution)/shard_map/all_to_all | solution.py:60
  16.8 1.1 broadcast_in_dim.23
  17.9 4.3 %all-to-all-start = ((bf16[32,8,2048]{2,1,0:T(8,128)(2,1)}), bf16[32,8,2048]{2,1,0:T(8,128)(2,1)}, u32[]{:S(2)}, u32[]{:S(2)}) async-start(bf16[32,8,2048]{2,1,0:T(8,128)(2,1)} %bitcast.67), calls=%async_computation | async-start | bytes 2097152 | tf_op jit(solution)/shard_map/all_to_all | solution.py:46
  22.1 0.0 copy-start.2
  22.2 2.8 %copy.25 = bf16[64,8192]{0,1:T(8,128)(2,1)} copy(bf16[64,8192]{1,0:T(8,128)(2,1)} %param.16) | data formatting | bytes 2097152 | tf_op args[7]
  24.9 2.8 %copy.27 = bf16[64,8192]{0,1:T(8,128)(2,1)} copy(bf16[64,8192]{1,0:T(8,128)(2,1)} %param.17) | data formatting | bytes 2097152 | tf_op args[8]
  27.7 0.0 copy-done.2
  27.7 3.9 %gather_fusion.1 = bf16[512,64,16]{1,2,0:T(8,128)(2,1)} fusion(bf16[64,512,16]{0,2,1:T(8,128)(2,1)} %bitcast.65, s32[1024]{0:T(1024)S(1)} %pad_clamp_fusion), kind=kCustom, calls=%fused_computation.1 | custom fusion | bytes 2099200 | tf_op jit(solution)/shard_map/gather | solution.py:63
  31.6 4.0 %gather_fusion.2 = bf16[512,64,16]{1,2,0:T(8,128)(2,1)} fusion(bf16[64,512,16]{0,2,1:T(8,128)(2,1)} %bitcast.64, s32[1024]{0:T(1024)S(1)} %pad_clamp_fusion), kind=kCustom, calls=%fused_computation.2 | custom fusion | bytes 2099200 | tf_op jit(solution)/shard_map/gather | solution.py:70
  35.6 0.1 reshape.133
  35.8 2.8 %fusion.11 = f32[512,1,16]{2,1,0:T(1,128)S(1)} fusion(bf16[512,64,16]{1,2,0:T(8,128)(2,1)} %gather_fusion.1, bf16[512,64,1]{1,0,2:T(8,128)(2,1)S(1)} %bitcast.74), kind=kOutput, calls=%fused_computation.14 | convolution fusion | flops 1048576 | bytes 1146880 | tf_op jit(solution)/shard_map/tf,ftr->tr/dot_general | solution.py:66
  38.5 43.0 %psum.7 = bf16[512,16]{1,0:T(8,128)(2,1)S(1)} all-reduce(f32[512,16]{1,0:T(8,128)S(1)} %bitcast.71), channel_id=1, replica_groups=mesh['grp'=1,'exp'=32] {'exp'}, use_global_device_ids=true, to_apply=%region_5.6 | all-reduce | flops 8192 | bytes 49152 | tf_op jit(solution)/shard_map/psum | solution.py:69
  81.6 2.3 %fusion.9 = f32[512,1,64]{2,1,0:T(1,128)S(1)} fusion(bf16[512,64,16]{1,2,0:T(8,128)(2,1)} %gather_fusion.2, bf16[512,16,1]{1,0,2:T(8,128)(2,1)S(1)} %bitcast.73), kind=kOutput, calls=%fused_computation.12 | convolution fusion | flops 1048576 | bytes 1196032 | tf_op jit(solution)/shard_map/tr,ftr->tf/dot_general | solution.py:73
  83.9 0.8 reshape.134
  84.6 0.0 all-to-all-done
  84.6 3.9 %all-to-all-start.3 = ((bf16[32,2,512]{2,1,0:T(2,128)(2,1)}), bf16[32,2,512]{2,1,0:T(2,128)(2,1)S(1)}, u32[]{:S(2)}, u32[]{:S(2)}) async-start(bf16[32,2,512]{2,1,0:T(2,128)(2,1)} %reshape.134), calls=%async_computation.3 | async-start | bytes 131072 | tf_op jit(solution)/shard_map/all_to_all | solution.py:76
  88.5 0.0 copy-start.3
  88.5 3.2 %fusion.4 = f32[256,704]{0,1:T(8,128)S(1)} fusion(bf16[1,2048,704]{1,2,0:T(8,128)(2,1)} %param.13, bf16[32,8,2048]{2,1,0:T(8,128)(2,1)} %all-to-all-done), kind=kOutput, calls=%fused_computation.8 | convolution fusion | flops 738197504 | bytes 4653056 | tf_op jit(solution)/shard_map/dot_general | solution.py:11
  91.8 0.0 copy-done.3
  91.8 2.9 %fusion.16 = bf16[256,704]{0,1:T(8,128)(2,1)} fusion(bf16[1,2048,704]{1,2,0:T(8,128)(2,1)S(1)} %copy-done.3, bf16[32,8,2048]{2,1,0:T(8,128)(2,1)} %all-to-all-done, f32[256,704]{0,1:T(8,128)S(1)} %fusion.4), kind=kOutput, calls=%fused_computation.17 | convolution fusion | flops 739278848 | bytes 5013504 | tf_op jit(solution)/shard_map/dot_general | solution.py:12
  94.7 1.2 copy.23
  95.8 0.0 copy-done
  95.8 0.0 copy-start.1
  95.9 2.0 %fusion.6 = bf16[32,8,2048]{2,1,0:T(8,128)(2,1)} fusion(bf16[1,704,2048]{2,1,0:T(8,128)(2,1)S(1)} %copy-done, bf16[256,704]{1,0:T(8,128)(2,1)S(1)} %copy.23), kind=kOutput, calls=%fused_computation.10 | convolution fusion | flops 738721792 | bytes 4292608 | tf_op jit(solution)/shard_map/dot_general | solution.py:14
  97.9 0.0 all-to-all-done.3
  97.9 6.0 %all-to-all-start.1 = ((bf16[32,8,2048]{2,1,0:T(8,128)(2,1)}), bf16[32,8,2048]{2,1,0:T(8,128)(2,1)}, u32[]{:S(2)}, u32[]{:S(2)}) async-start(bf16[32,8,2048]{2,1,0:T(8,128)(2,1)} %fusion.6), calls=%async_computation.1 | async-start | bytes 2097152 | tf_op jit(solution)/shard_map/all_to_all | solution.py:53
  103.9 0.0 copy-done.1
  103.9 0.1 copy.24
  104.0 0.1 reshape.135
  104.1 0.1 copy.28
  104.2 0.1 reshape.90
  104.3 25.7 %all-to-all-done.1 = bf16[32,8,2048]{2,1,0:T(8,128)(2,1)} async-done(((bf16[32,8,2048]{2,1,0:T(8,128)(2,1)}), bf16[32,8,2048]{2,1,0:T(8,128)(2,1)}, u32[]{:S(2)}, u32[]{:S(2)}) %all-to-all-start.1) | async-done | bytes 1048608 | tf_op jit(solution)/shard_map/all_to_all | solution.py:53
  130.0 2.5 %convert_reduce_fusion = f32[16,8,2048]{2,1,0:T(8,128)} fusion(bf16[32,8,2048]{2,1,0:T(8,128)(2,1)} %all-to-all-done.1), kind=kLoop, calls=%fused_computation.11 | loop fusion | flops 786432 | bytes 2097152 | tf_op jit(solution)/shard_map/reduce_sum | solution.py:56
  132.6 3.3 %gather_fusion = f32[96,2048]{1,0:T(8,128)} fusion(f32[128,2048]{1,0:T(8,128)} %bitcast.66, s32[1024]{0:T(1024)S(1)} %pad_clamp_fusion.1), kind=kCustom, calls=%fused_computation | custom fusion | bytes 1573248 | tf_op jit(solution)/shard_map/gather | solution.py:58
  135.9 2.2 %gather.12 = f32[16,6,2048]{2,1,0:T(8,128)} reshape(f32[96,2048]{1,0:T(8,128)} %gather_fusion) | data formatting | bytes 1572864 | tf_op jit(solution)/shard_map/gather | solution.py:58
  138.1 1.6 %multiply_reduce_fusion = f32[16,2048]{1,0:T(8,128)S(1)} fusion(f32[16,6,2048]{2,1,0:T(8,128)} %gather.12, f32[16,6]{1,0:T(8,128)S(1)} %copy.24), kind=kLoop, calls=%fused_computation.20 | loop fusion | flops 360448 | bytes 917888 | tf_op jit(solution)/shard_map/reduce_sum | solution.py:59
  139.7 0.6 add_convert_fusion
  (6 shorter events, 0.1 us)
Async XLA Ops:
  0.0 95.8 %copy-start = (bf16[1,704,2048]{2,1,0:T(8,128)(2,1)S(1)}, bf16[1,704,2048]{2,1,0:T(8,128)(2,1)}, u32[]{:S(2)}) copy-start(bf16[1,704,2048]{2,1,0:T(8,128)(2,1)} %param.15) | copy-start | bytes 8650756
  2.0 14.7 %all-to-all-start.2 = ((bf16[32,2,512]{2,1,0:T(2,128)(2,1)}), bf16[32,2,512]{2,1,0:T(2,128)(2,1)S(1)}, u32[]{:S(2)}, u32[]{:S(2)}) async-start(bf16[32,2,512]{2,1,0:T(2,128)(2,1)} %reshape.132), calls=%async_computation.2 | async-start | bytes 131072 | tf_op jit(solution)/shard_map/all_to_all | solution.py:60
  17.9 66.8 %all-to-all-start = ((bf16[32,8,2048]{2,1,0:T(8,128)(2,1)}), bf16[32,8,2048]{2,1,0:T(8,128)(2,1)}, u32[]{:S(2)}, u32[]{:S(2)}) async-start(bf16[32,8,2048]{2,1,0:T(8,128)(2,1)} %bitcast.67), calls=%async_computation | async-start | bytes 2097152 | tf_op jit(solution)/shard_map/all_to_all | solution.py:46
  22.1 5.6 %copy-start.2 = (s32[512]{0:T(512)S(1)}, s32[512]{0:T(512)}, u32[]{:S(2)}) copy-start(s32[512]{0:T(512)} %param.12) | copy-start | bytes 6148
  84.6 13.3 %all-to-all-start.3 = ((bf16[32,2,512]{2,1,0:T(2,128)(2,1)}), bf16[32,2,512]{2,1,0:T(2,128)(2,1)S(1)}, u32[]{:S(2)}, u32[]{:S(2)}) async-start(bf16[32,2,512]{2,1,0:T(2,128)(2,1)} %reshape.134), calls=%async_computation.3 | async-start | bytes 131072 | tf_op jit(solution)/shard_map/all_to_all | solution.py:76
  88.5 3.3 %copy-start.3 = (bf16[1,2048,704]{1,2,0:T(8,128)(2,1)S(1)}, bf16[1,2048,704]{1,2,0:T(8,128)(2,1)}, u32[]{:S(2)}) copy-start(bf16[1,2048,704]{1,2,0:T(8,128)(2,1)} %param.14) | copy-start | bytes 8650756
  95.8 8.0 %copy-start.1 = (f32[16,6]{0,1:T(8,128)S(1)}, f32[16,6]{0,1:T(8,128)}, u32[]{:S(2)}) copy-start(f32[16,6]{0,1:T(8,128)} %param.11) | copy-start | bytes 1156
  97.9 32.1 %all-to-all-start.1 = ((bf16[32,8,2048]{2,1,0:T(8,128)(2,1)}), bf16[32,8,2048]{2,1,0:T(8,128)(2,1)}, u32[]{:S(2)}, u32[]{:S(2)}) async-start(bf16[32,8,2048]{2,1,0:T(8,128)(2,1)} %fusion.6), calls=%async_computation.1 | async-start | bytes 2097152 | tf_op jit(solution)/shard_map/all_to_all | solution.py:53
where the time goes:
time: 141 us; the launch traced here: 140 us
  blocking collectives  43 us (30%)
  local copies, waits for them, and re-layouts  29.2 us (21%)
  waiting for transfers between devices  27.4 us (19%)
  starting transfers between devices  21.4 us (15%)
  matrix products  13.2 us (9%)
  other arithmetic  5.94 us (4%)
    psum x1, blocking collectives, per_device(): gathered_ranks = lax.psum(rank_terms, 'exp').astype(jnp.bfloat16)  43 us
    all_to_all x1, waiting for transfers between devices, per_device(): lax.all_to_all(partial_value.astype(jnp.bfloat16), 'exp', split_axis=0, c...  25.7 us
    unnamed x16, local copies, waits for them, and re-layouts  8.22 us
    all_to_all x1, starting transfers between devices, per_device(): lax.all_to_all(tokens, 'exp', split_axis=1, concat_axis=0, tiled=True)  7.33 us
    all_to_all x1, starting transfers between devices, per_device(): lax.all_to_all(partial_value.astype(jnp.bfloat16), 'exp', split_axis=0, c...  5.96 us
    gather x2, local copies, waits for them, and re-layouts, per_device(): picked = gather_results[slots] * gate_col  5.55 us
    all_to_all x1, starting transfers between devices, per_device(): lax.all_to_all(doubled, 'exp', split_axis=0, concat_axis=0, tiled=True)  4.27 us
    gather x1, local copies, waits for them, and re-layouts, per_device(): adapter_up_matrix.reshape(feature_rows, adapter_table, ADAPTER_RANK)  3.97 us
  transfers between devices with their start and end apart: 4, of which 2 were waited for; matrix products, arithmetic and copies ran while one was open for 25% of the time, Pallas kernels for 0%

commit v1 on v0

--- a/solution.py
+++ b/solution.py
@@ -5,6 +5,7 @@
 
 TOP = 6
 ADAPTER_RANK = 16
+members_all_review = lambda inner_x: jnp.sum(lax.all_gather(inner_x, "exp"), 0)
 
 
 def expert_half(row_block, gate_weight_pieces, up_weight, down_weight):
@@ -66,7 +67,7 @@
     rank_terms = jnp.einsum(
         "tf,ftr->tr", columns, down_selected, preferred_element_type=jnp.float32
     )
-    gathered_ranks = lax.psum(rank_terms, "exp").astype(jnp.bfloat16)
+    gathered_ranks = members_all_review(rank_terms).astype(jnp.bfloat16)
     up_selected = adapter_up_matrix.reshape(feature_rows, adapter_table, ADAPTER_RANK)[
         :, token_adapter_index, :
     ]

time: 141 us -> 159 us (1.13)
  waiting for transfers between devices: 27.4 us -> 73.6 us
  blocking collectives: 43 us -> 0 us
  between operations: 0.22 us -> 13.6 us
  local copies, waits for them, and re-layouts: 29.2 us -> 32.7 us
  starting transfers between devices: 21.4 us -> 18.6 us
    psum x1 -> x0, blocking collectives: 43 us -> none  [per_device(): gathered_ranks = lax.psum(rank_terms, 'exp').astype(jnp.bfloat16)]
    all_gather x0 -> x1, waiting for transfers between devices: none -> 31.6 us  [lax.all_gather(inner_x, 'exp')]
    all_to_all x1, waiting for transfers between devices: 0.01 us -> 9.21 us  [per_device(): lax.all_to_all(doubled, 'exp', split_axis=0, concat_axis=0, tiled=True)]
    all_to_all x1, waiting for transfers between devices: 0.01 us -> 5.36 us  [per_device(): lax.all_to_all(correction_cols.astype(jnp.bfloat16), 'exp', split_axis=0,...]
    all_to_all x1, starting transfers between devices: 5.96 us -> 3.38 us  [per_device(): lax.all_to_all(partial_value.astype(jnp.bfloat16), 'exp', split_axis=0, c...]
    unnamed x16 -> x17, local copies, waits for them, and re-layouts: 8.22 us -> 10 us
  transfers between devices with their start and end apart: 4 -> 5, of which waited for: 2 -> 5; matrix products, arithmetic and copies ran while one was open for 25% -> 21% of each run, Pallas kernels for 0% -> 0%
where the time goes in v1:
time: 159 us; the launch traced here: 158 us
  waiting for transfers between devices  73.6 us (46%)
  local copies, waits for them, and re-layouts  32.7 us (21%)
  starting transfers between devices  18.6 us (12%)
  between operations  13.6 us (9%)
  matrix products  13.3 us (8%)
  other arithmetic  6.04 us (4%)
    all_gather x1, waiting for transfers between devices, lax.all_gather(inner_x, 'exp')  31.6 us
    all_to_all x1, waiting for transfers between devices, per_device(): lax.all_to_all(partial_value.astype(jnp.bfloat16), 'exp', split_axis=0, c...  25.7 us
    unnamed x17, local copies, waits for them, and re-layouts  10 us
    all_to_all x1, waiting for transfers between devices, per_device(): lax.all_to_all(doubled, 'exp', split_axis=0, concat_axis=0, tiled=True)  9.21 us
    all_to_all x1, starting transfers between devices, per_device(): lax.all_to_all(tokens, 'exp', split_axis=1, concat_axis=0, tiled=True)  7.33 us
    gather x2, local copies, waits for them, and re-layouts, per_device(): picked = gather_results[slots] * gate_col  5.55 us
    all_to_all x1, waiting for transfers between devices, per_device(): lax.all_to_all(correction_cols.astype(jnp.bfloat16), 'exp', split_axis=0,...  5.36 us
    all_to_all x1, starting transfers between devices, per_device(): lax.all_to_all(doubled, 'exp', split_axis=0, concat_axis=0, tiled=True)  4.27 us
  transfers between devices with their start and end apart: 5, of which 5 were waited for; matrix products, arithmetic and copies ran while one was open for 21% of the time, Pallas kernels for 0%

profile of v1, /device:TPU:0, one launch (start us, length us, event | category | flops | bytes accessed | tf_op | source)
XLA Modules:
  0.0 157.8 jit_solution(2687017034624206270)
XLA Ops:
  6.5 0.0 copy-start
  6.5 1.2 all_to_all.32
  7.7 0.1 copy.47
  7.8 0.8 reshape.133
  8.5 7.3 %all-to-all-start.2 = ((bf16[32,2,512]{2,1,0:T(2,128)(2,1)}), bf16[32,2,512]{2,1,0:T(2,128)(2,1)S(1)}, u32[]{:S(2)}, u32[]{:S(2)}) async-start(bf16[32,2,512]{2,1,0:T(2,128)(2,1)} %reshape.133), calls=%async_computation.2 | async-start | bytes 131072 | tf_op jit(solution)/shard_map/all_to_all | solution.py:61
  15.9 0.7 broadcast_multiply_fusion
  16.6 0.8 copy.30
  17.3 0.1 copy.29
  17.4 0.1 mul.37
  17.5 0.1 eq.15
  17.6 0.1 fusion.25
  17.7 0.1 reduce_window_sum.11
  17.8 0.2 select_reduce_fusion
  18.0 0.9 broadcast_in_dim.21
  18.9 0.9 reshape.119
  19.8 1.8 %scatter_custom_fusion = bf16[128,2048]{1,0:T(8,128)(2,1)S(1)} fusion(s32[96]{0:T(128)S(1)} %fusion.26, bf16[96,2048]{1,0:T(8,128)(2,1)} %reshape.119, bf16[]{:T(256)} %constant.8.clone.1), kind=kCustom, calls=%fused_computation.25 | custom fusion | bytes 524800 | tf_op jit(solution)/shard_map/scatter | solution.py:41
  21.6 1.7 %all-to-all-done.2 = bf16[32,2,512]{2,1,0:T(2,128)(2,1)S(1)} async-done(((bf16[32,2,512]{2,1,0:T(2,128)(2,1)}), bf16[32,2,512]{2,1,0:T(2,128)(2,1)S(1)}, u32[]{:S(2)}, u32[]{:S(2)}) %all-to-all-start.2) | async-done | bytes 65568 | tf_op jit(solution)/shard_map/all_to_all | solution.py:61
  23.3 1.1 broadcast_in_dim.23
  24.4 0.0 copy-start.2
  24.4 4.3 %all-to-all-start = ((bf16[32,8,2048]{2,1,0:T(8,128)(2,1)}), bf16[32,8,2048]{2,1,0:T(8,128)(2,1)}, u32[]{:S(2)}, u32[]{:S(2)}) async-start(bf16[32,8,2048]{2,1,0:T(8,128)(2,1)} %bitcast.72), calls=%async_computation | async-start | bytes 2097152 | tf_op jit(solution)/shard_map/all_to_all | solution.py:47
  28.7 0.0 all-gather.3.cloned.1.call-start
  28.8 2.8 %copy.33 = bf16[64,8192]{0,1:T(8,128)(2,1)} copy(bf16[64,8192]{1,0:T(8,128)(2,1)} %param.16) | data formatting | bytes 2097152 | tf_op args[7]
  31.6 0.0 copy-done.2
  31.6 3.9 %gather_fusion.1 = bf16[512,64,16]{1,2,0:T(8,128)(2,1)} fusion(bf16[64,512,16]{0,2,1:T(8,128)(2,1)} %bitcast.69, s32[1024]{0:T(1024)S(1)} %pad_clamp_fusion), kind=kCustom, calls=%fused_computation.1 | custom fusion | bytes 2099200 | tf_op jit(solution)/shard_map/gather | solution.py:64
  35.5 0.1 reshape.134
  35.6 2.8 %fusion.11 = f32[512,1,16]{2,1,0:T(1,128)S(1)} fusion(bf16[512,64,16]{1,2,0:T(8,128)(2,1)} %gather_fusion.1, bf16[512,64,1]{1,0,2:T(8,128)(2,1)S(1)} %bitcast.79), kind=kOutput, calls=%fused_computation.14 | convolution fusion | flops 1048576 | bytes 1146880 | tf_op jit(solution)/shard_map/tf,ftr->tr/dot_general | solution.py:67
  38.4 0.7 copy.39
  39.2 0.0 all-gather.3.cloned.1.call-update
  39.2 2.7 %copy.36 = bf16[64,8192]{0,1:T(8,128)(2,1)} copy(bf16[64,8192]{1,0:T(8,128)(2,1)} %param.17) | data formatting | bytes 2097152 | tf_op args[8]
  41.9 4.0 %gather_fusion.2 = bf16[512,64,16]{1,2,0:T(8,128)(2,1)} fusion(bf16[64,512,16]{0,2,1:T(8,128)(2,1)} %bitcast.70, s32[1024]{0:T(1024)S(1)} %pad_clamp_fusion), kind=kCustom, calls=%fused_computation.2 | custom fusion | bytes 2099200 | tf_op jit(solution)/shard_map/gather | solution.py:71
  45.9 9.2 %all-to-all-done = bf16[32,8,2048]{2,1,0:T(8,128)(2,1)} async-done(((bf16[32,8,2048]{2,1,0:T(8,128)(2,1)}), bf16[32,8,2048]{2,1,0:T(8,128)(2,1)}, u32[]{:S(2)}, u32[]{:S(2)}) %all-to-all-start) | async-done | bytes 1048608 | tf_op jit(solution)/shard_map/all_to_all | solution.py:47
  55.1 0.0 copy-start.3
  55.1 3.2 %fusion.4 = f32[256,704]{0,1:T(8,128)S(1)} fusion(bf16[1,2048,704]{1,2,0:T(8,128)(2,1)} %param.13, bf16[32,8,2048]{2,1,0:T(8,128)(2,1)} %all-to-all-done), kind=kOutput, calls=%fused_computation.8 | convolution fusion | flops 738197504 | bytes 4653056 | tf_op jit(solution)/shard_map/dot_general | solution.py:12
  58.4 0.0 copy-done.3
  58.4 2.9 %fusion.16 = bf16[256,704]{0,1:T(8,128)(2,1)} fusion(bf16[1,2048,704]{1,2,0:T(8,128)(2,1)S(1)} %copy-done.3, bf16[32,8,2048]{2,1,0:T(8,128)(2,1)} %all-to-all-done, f32[256,704]{0,1:T(8,128)S(1)} %fusion.4), kind=kOutput, calls=%fused_computation.17 | convolution fusion | flops 739278848 | bytes 5013504 | tf_op jit(solution)/shard_map/dot_general | solution.py:13
  61.3 1.2 copy.31
  62.4 31.6 %all-gather.3.cloned.1.call-done = f32[16384,16]{0,1:T(8,128)} async-done(((f32[512,16]{0,1:T(8,128)}), f32[16384,16]{0,1:T(8,128)}) %all-gather.3.cloned.1.call-update) | async-done | bytes 1048592 | tf_op jit(solution)/shard_map/all_gather | solution.py:8
  94.0 1.8 %copy.43 = f32[2,8,32,512]{3,2,1,0:T(8,128)S(1)} copy(f32[2,8,32,512]{3,1,2,0:T(8,128)} %bitcast.74) | data formatting | bytes 2097152
  95.9 0.1 bitcast_reduce_fusion
  96.0 0.9 copy.40
  96.9 2.4 %fusion.9 = f32[512,1,64]{2,1,0:T(1,128)S(1)} fusion(bf16[512,16,1]{1,2,0:T(2,128)(2,1)} %copy.40, bf16[512,64,16]{1,2,0:T(8,128)(2,1)} %gather_fusion.2), kind=kOutput, calls=%fused_computation.12 | convolution fusion | flops 1048576 | bytes 1196032 | tf_op jit(solution)/shard_map/tr,ftr->tf/dot_general | solution.py:74
  99.3 0.8 reshape.135
  100.0 3.6 %all-to-all-start.3 = ((bf16[32,2,512]{2,1,0:T(2,128)(2,1)}), bf16[32,2,512]{2,1,0:T(2,128)(2,1)S(1)}, u32[]{:S(2)}, u32[]{:S(2)}) async-start(bf16[32,2,512]{2,1,0:T(2,128)(2,1)} %reshape.135), calls=%async_computation.3 | async-start | bytes 131072 | tf_op jit(solution)/shard_map/all_to_all | solution.py:77
  103.7 0.0 copy-done
  103.7 0.0 copy-start.1
  103.7 2.0 %fusion.6 = bf16[32,8,2048]{2,1,0:T(8,128)(2,1)} fusion(bf16[1,704,2048]{2,1,0:T(8,128)(2,1)S(1)} %copy-done, bf16[256,704]{1,0:T(8,128)(2,1)S(1)} %copy.31), kind=kOutput, calls=%fused_computation.10 | convolution fusion | flops 738721792 | bytes 4292608 | tf_op jit(solution)/shard_map/dot_general | solution.py:15
  105.7 5.4 %all-to-all-done.3 = bf16[32,2,512]{2,1,0:T(2,128)(2,1)S(1)} async-done(((bf16[32,2,512]{2,1,0:T(2,128)(2,1)}), bf16[32,2,512]{2,1,0:T(2,128)(2,1)S(1)}, u32[]{:S(2)}, u32[]{:S(2)}) %all-to-all-start.3) | async-done | bytes 65568 | tf_op jit(solution)/shard_map/all_to_all | solution.py:77
  111.1 3.4 %all-to-all-start.1 = ((bf16[32,8,2048]{2,1,0:T(8,128)(2,1)}), bf16[32,8,2048]{2,1,0:T(8,128)(2,1)}, u32[]{:S(2)}, u32[]{:S(2)}) async-start(bf16[32,8,2048]{2,1,0:T(8,128)(2,1)} %fusion.6), calls=%async_computation.1 | async-start | bytes 2097152 | tf_op jit(solution)/shard_map/all_to_all | solution.py:54
  114.5 0.0 copy-done.1
  114.5 0.1 copy.32
  114.6 0.1 reshape.136
  114.7 0.1 copy.37
  114.8 0.1 reshape.90
  114.9 25.7 %all-to-all-done.1 = bf16[32,8,2048]{2,1,0:T(8,128)(2,1)} async-done(((bf16[32,8,2048]{2,1,0:T(8,128)(2,1)}), bf16[32,8,2048]{2,1,0:T(8,128)(2,1)}, u32[]{:S(2)}, u32[]{:S(2)}) %all-to-all-start.1) | async-done | bytes 1048608 | tf_op jit(solution)/shard_map/all_to_all | solution.py:54
  140.6 2.5 %convert_reduce_fusion = f32[16,8,2048]{2,1,0:T(8,128)} fusion(bf16[32,8,2048]{2,1,0:T(8,128)(2,1)} %all-to-all-done.1), kind=kLoop, calls=%fused_computation.11 | loop fusion | flops 786432 | bytes 2097152 | tf_op jit(solution)/shard_map/reduce_sum | solution.py:57
  143.2 3.3 %gather_fusion = f32[96,2048]{1,0:T(8,128)} fusion(f32[128,2048]{1,0:T(8,128)} %bitcast.71, s32[1024]{0:T(1024)S(1)} %pad_clamp_fusion.1), kind=kCustom, calls=%fused_computation | custom fusion | bytes 1573248 | tf_op jit(solution)/shard_map/gather | solution.py:59
  146.5 2.2 %gather.12 = f32[16,6,2048]{2,1,0:T(8,128)} reshape(f32[96,2048]{1,0:T(8,128)} %gather_fusion) | data formatting | bytes 1572864 | tf_op jit(solution)/shard_map/gather | solution.py:59
  148.7 1.6 %multiply_reduce_fusion = f32[16,2048]{1,0:T(8,128)S(1)} fusion(f32[16,6,2048]{2,1,0:T(8,128)} %gather.12, f32[16,6]{1,0:T(8,128)S(1)} %copy.32), kind=kLoop, calls=%fused_computation.21 | loop fusion | flops 360448 | bytes 917888 | tf_op jit(solution)/shard_map/reduce_sum | solution.py:60
  150.3 0.6 add_convert_fusion
  (6 shorter events, 0.1 us)
Async XLA Ops:
  6.5 97.1 %copy-start = (bf16[1,704,2048]{2,1,0:T(8,128)(2,1)S(1)}, bf16[1,704,2048]{2,1,0:T(8,128)(2,1)}, u32[]{:S(2)}) copy-start(bf16[1,704,2048]{2,1,0:T(8,128)(2,1)} %param.15) | copy-start | bytes 8650756
  8.5 14.7 %all-to-all-start.2 = ((bf16[32,2,512]{2,1,0:T(2,128)(2,1)}), bf16[32,2,512]{2,1,0:T(2,128)(2,1)S(1)}, u32[]{:S(2)}, u32[]{:S(2)}) async-start(bf16[32,2,512]{2,1,0:T(2,128)(2,1)} %reshape.133), calls=%async_computation.2 | async-start | bytes 131072 | tf_op jit(solution)/shard_map/all_to_all | solution.py:61
  24.4 7.1 %copy-start.2 = (s32[512]{0:T(512)S(1)}, s32[512]{0:T(512)}, u32[]{:S(2)}) copy-start(s32[512]{0:T(512)} %param.12) | copy-start | bytes 6148
  24.4 30.7 %all-to-all-start = ((bf16[32,8,2048]{2,1,0:T(8,128)(2,1)}), bf16[32,8,2048]{2,1,0:T(8,128)(2,1)}, u32[]{:S(2)}, u32[]{:S(2)}) async-start(bf16[32,8,2048]{2,1,0:T(8,128)(2,1)} %bitcast.72), calls=%async_computation | async-start | bytes 2097152 | tf_op jit(solution)/shard_map/all_to_all | solution.py:47
  28.7 65.3 %all-gather.3.cloned.1.call-start = ((), (), s32[]{:S(2)}) async-start(), calls=%async_computation.4 | async-start | bytes 1081344 | tf_op jit(solution)/shard_map/all_gather | solution.py:8
  55.1 3.2 %copy-start.3 = (bf16[1,2048,704]{1,2,0:T(8,128)(2,1)S(1)}, bf16[1,2048,704]{1,2,0:T(8,128)(2,1)}, u32[]{:S(2)}) copy-start(bf16[1,2048,704]{1,2,0:T(8,128)(2,1)} %param.14) | copy-start | bytes 8650756
  100.0 11.0 %all-to-all-start.3 = ((bf16[32,2,512]{2,1,0:T(2,128)(2,1)}), bf16[32,2,512]{2,1,0:T(2,128)(2,1)S(1)}, u32[]{:S(2)}, u32[]{:S(2)}) async-start(bf16[32,2,512]{2,1,0:T(2,128)(2,1)} %reshape.135), calls=%async_computation.3 | async-start | bytes 131072 | tf_op jit(solution)/shard_map/all_to_all | solution.py:77
  103.7 10.8 %copy-start.1 = (f32[16,6]{0,1:T(8,128)S(1)}, f32[16,6]{0,1:T(8,128)}, u32[]{:S(2)}) copy-start(f32[16,6]{0,1:T(8,128)} %param.11) | copy-start | bytes 1156
  111.1 29.6 %all-to-all-start.1 = ((bf16[32,8,2048]{2,1,0:T(8,128)(2,1)}), bf16[32,8,2048]{2,1,0:T(8,128)(2,1)}, u32[]{:S(2)}, u32[]{:S(2)}) async-start(bf16[32,8,2048]{2,1,0:T(8,128)(2,1)} %fusion.6), calls=%async_computation.1 | async-start | bytes 2097152 | tf_op jit(solution)/shard_map/all_to_all | solution.py:54
Sparse Core Ops, SparseCore 0:
  39.3 54.6 all-gather.2
